TPU v7x, 128 devices: a whole 4x4x4 slice. The times are simulated.
128 devices in a mesh: space: 8 (over z_lo, x), mode: 16 (over z_hi, y, core).
Axes of the slice: x: 4, y: 4, z: 4 (z_hi: 2, z_lo: 2; z = z_hi * 2 + z_lo), core: 2. Of those that a mesh axis runs over, the one named last changes fastest.
Arguments:
- excess_phonon_enthalpy: bfloat16 [768, 64, 128, 128], P('mode', 'space'), may hold values from -0.21972656 to 0.21972656
- thermal_offset: float32 [128, 128, 64], P('space', 'mode'), may hold values from -6 to 6
- state_specific_warmth_scaled: float32 [768], P('mode'), may hold values from 0.5 to 2
- scattering_lifetimes: float32 [768], P('mode'), may hold values from 0.5 to 50
- state_polarization_label: int32 [768], P('mode'), may hold values from 0 to 5
- state_orientation_label: int32 [768], P('mode'), may hold values from 0 to 15
- polarization_propagation_rate: float32 [6], replicated, may hold values from 0.3 to 1
- thermal_conductance_bulk: float32 [128, 128, 64], P('space', 'mode'), may hold values from 0.25 to 1
- substance_label: int32 [128, 128, 64], P('space', 'mode'), may hold values 0 or 1
Outputs:
- final_temperature: float32 [128, 128, 64], P('space', 'mode')
- heat_flux: float32 [3, 128, 128, 64], P(None, 'space', 'mode')
Inputs may be any that keep to these rules, and one draw needn't show every extreme that they name: `substance_label`: 1 marks a pore cell.
All inputs are finite; a program needn't handle non-finite values. No bound on the sum of `substance_label` on one device may be relied on, other than what follows from the above.
Results may differ from a plain program's by a relative error of at most 0.0028.
Values may be sent and summed in bfloat16 or wider, within the bound.
No kernel may reach another device: no remote copies, remote signals or barrier semaphores. Data moves between devices by JAX's collectives and lax.ppermute only.
A program may use at most 128 MiB of HBM per device.

v0:
```python
import math
import jax
import jax.numpy as jnp
from jax import lax
from jax.sharding import PartitionSpec as P

M = 768
SWEEPS = 4
OUTER = 2
time_step = 0.25
pore_factor = 0.1
kappa_top = 1.0


def padded_2(cells, sides, width):
    for axis, dim in sides:
        count = lax.axis_size(axis)
        ends = count - 1
        head = lax.slice_in_dim(cells, 0, width, axis=dim)
        tail = lax.slice_in_dim(cells, cells.shape[dim] - width, cells.shape[dim], axis=dim)
        cells = jnp.concatenate(
            [
                lax.ppermute(tail, axis, [(i, (i + 1) % count) for i in range(ends)]),
                cells,
                lax.ppermute(head, axis, [((i + 1) % count, i) for i in range(ends)]),
            ],
            axis=dim,
        )
    return cells


def sent_to_all(shard, axis):
    copies = jnp.broadcast_to(shard, (lax.axis_size(axis), *shard.shape))
    return lax.all_to_all(copies, axis, split_axis=0, concat_axis=0, tiled=True)


def over_copies(shard, axis):
    everything = sent_to_all(shard, axis)
    return jnp.sum(everything, axis=0)


def in_blocks(shard, dim, length):
    before, after = (shard.shape[:dim], shard.shape[dim + 1 :])
    return jnp.moveaxis(shard.reshape(*before, length, -1, *after), dim, 0)


def sum_at_owner(shard, axis, dim):
    length = lax.axis_size(axis)
    pieces = lax.all_to_all(in_blocks(shard, dim, length), axis, 0, 0, tiled=True)
    return jnp.sum(pieces, axis=0)


def mode_table(
    state_polarization_label,
    state_orientation_label,
    state_specific_warmth_scaled,
    scattering_lifetimes,
    polarization_propagation_rate,
):
    branches = jnp.arange(polarization_propagation_rate.shape[0], dtype=jnp.int32)
    onehot = (state_polarization_label[:, None] == branches[None, :]).astype(jnp.float32)
    speed = jnp.sum(onehot * polarization_propagation_rate[None, :], axis=1)
    polar = state_orientation_label // 4
    azimuth = state_orientation_label % 4
    cosine = (2 * polar + 1).astype(jnp.float32) * 0.25 - 1.0
    sine = jnp.sqrt(1.0 - cosine * cosine)
    angle = (azimuth.astype(jnp.float32) + 0.5) * (math.pi / 2.0)
    velocity = (speed * sine * jnp.cos(angle), speed * sine * jnp.sin(angle), speed * cosine)
    rates = 1.0 / scattering_lifetimes
    capacity = state_specific_warmth_scaled / float(M)
    return (velocity, rates, capacity)


def upwind(padded, temp_slab, along_x, along_y, along_z, rates, capacity):

    def widen(values):
        return values[:, None, None, None]

    current = padded[:, 1:-1]
    z_before = padded[:, :-2]
    z_after = padded[:, 2:]
    x_padded = jnp.pad(current, ((0, 0), (0, 0), (1, 1), (0, 0)))
    y_padded = jnp.pad(current, ((0, 0), (0, 0), (0, 0), (1, 1)))

    def advect(speed, before, after):
        flow = widen(speed)
        return jnp.maximum(flow, 0.0) * (current - before) + jnp.minimum(flow, 0.0) * (
            after - current
        )

    total_advect = advect(along_x, x_padded[:, :, :-2], x_padded[:, :, 2:])
    total_advect = total_advect + advect(along_y, y_padded[:, :, :, :-2], y_padded[:, :, :, 2:])
    total_advect = total_advect + advect(along_z, z_before, z_after)
    updated = (
        current
        - time_step * total_advect
        + time_step * widen(rates) * (widen(capacity) * temp_slab[None] - current)
    )
    weights = jnp.stack([rates, along_x, along_y, along_z])
    moments = jnp.einsum("km,mzxy->kzxy", weights, updated, precision=lax.Precision.HIGHEST)
    return (updated, moments)


def harmonic(first, second):
    summed = first + second
    positive = summed > 0.0
    return jnp.where(positive, 2.0 * first * second / jnp.where(positive, summed, 1.0), 0.0)


def face_table(kappa_ext):
    center = kappa_ext[1:-1, 1:-1]
    z_padded = jnp.pad(center, ((0, 0), (0, 0), (1, 1)))
    return (
        harmonic(center, kappa_ext[2:, 1:-1]),
        harmonic(kappa_ext[:-2, 1:-1], center),
        harmonic(center, kappa_ext[1:-1, 2:]),
        harmonic(kappa_ext[1:-1, :-2], center),
        harmonic(center, z_padded[:, :, 2:]),
        harmonic(z_padded[:, :, :-2], center),
    )


def crop(values, matrix_height, matrix_breadth):
    top = (values.shape[0] - matrix_height) // 2
    left = (values.shape[1] - matrix_breadth) // 2
    return values[top : top + matrix_height, left : left + matrix_breadth]


def apply_operator(padded, faces, total):
    matrix_height = padded.shape[0] - 2
    matrix_breadth = padded.shape[1] - 2
    cut = [crop(face, matrix_height, matrix_breadth) for face in faces]
    center = padded[1:-1, 1:-1]
    z_padded = jnp.pad(center, ((0, 0), (0, 0), (1, 1)))
    spread = cut[0] * (padded[2:, 1:-1] - center) + cut[1] * (padded[:-2, 1:-1] - center)
    spread = spread + cut[2] * (padded[1:-1, 2:] - center) + cut[3] * (padded[1:-1, :-2] - center)
    spread = (
        spread + cut[4] * (z_padded[:, :, 2:] - center) + cut[5] * (z_padded[:, :, :-2] - center)
    )
    return total * center - spread


def divergence(fluxes):
    z_flux = jnp.pad(fluxes[2][1:-1, 1:-1], ((0, 0), (0, 0), (1, 1)))
    summed = (
        fluxes[0][2:, 1:-1] - fluxes[0][:-2, 1:-1] + (fluxes[1][1:-1, 2:] - fluxes[1][1:-1, :-2])
    )
    summed = summed + (z_flux[:, :, 2:] - z_flux[:, :, :-2])
    return summed * 0.5


def chebyshev(rhs, faces, total, extend, matrix_height, matrix_breadth):
    theta = total + 6.0 * kappa_top
    spread = 6.0 * kappa_top
    sigma = theta / spread
    rho = 1.0 / sigma
    residual = rhs
    direction = rhs / theta
    correction = jnp.zeros((matrix_height, matrix_breadth, rhs.shape[2]), jnp.float32)
    for sweep in range(SWEEPS):
        correction = correction + crop(direction, matrix_height, matrix_breadth)
        if sweep < SWEEPS - 1:
            image = apply_operator(extend(direction), faces, total)
            residual = crop(residual, image.shape[0], image.shape[1]) - image
            rho_next = 1.0 / (2.0 * sigma - rho)
            direction = (
                rho_next * rho * crop(direction, image.shape[0], image.shape[1])
                + 2.0 * rho_next / spread * residual
            )
            rho = rho_next
    return correction


def unchanged(direction):
    return direction


def to_slab(block):
    upright = jnp.transpose(block, (2, 0, 1))
    moved = lax.all_to_all(upright, "space", split_axis=0, concat_axis=1, tiled=True)
    return lax.all_gather(moved, "mode", axis=2, tiled=True)


def kinetic(state, temp_slab, velocity, rates, capacity):
    padded = padded_2(state, (("space", 1),), 1)
    local = padded.shape[0]
    group = math.gcd(local, 8)
    count = local // group
    shaped = padded.reshape((count, group) + padded.shape[1:])
    params = (
        velocity[0].reshape(count, group),
        velocity[1].reshape(count, group),
        velocity[2].reshape(count, group),
        rates.reshape(count, group),
        capacity.reshape(count, group),
    )

    def step(carry, inputs):
        block, along_x, along_y, along_z, rate_part, cap_part = inputs
        updated, moments = upwind(
            block.astype(jnp.float32), temp_slab, along_x, along_y, along_z, rate_part, cap_part
        )
        return (carry + moments, updated.astype(jnp.bfloat16))

    start = jnp.zeros((4,) + state.shape[1:], jnp.float32)
    moments, news = lax.scan(step, start, (shaped,) + params)
    return (news.reshape(state.shape), moments)


def per_device(
    excess_phonon_enthalpy,
    thermal_offset,
    state_specific_warmth_scaled,
    scattering_lifetimes,
    state_polarization_label,
    state_orientation_label,
    polarization_propagation_rate,
    thermal_conductance_bulk,
    substance_label,
):
    velocity, rates, capacity = mode_table(
        state_polarization_label,
        state_orientation_label,
        state_specific_warmth_scaled,
        scattering_lifetimes,
        polarization_propagation_rate,
    )
    total = over_copies(jnp.sum(capacity * rates), "mode")
    kappa = thermal_conductance_bulk * jnp.where(substance_label == 1, pore_factor, 1.0)
    matrix_height = thermal_offset.shape[0]
    matrix_breadth = thermal_offset.shape[1]
    kappa_ext = padded_2(kappa.astype(jnp.bfloat16), (("space", 0), ("mode", 1)), SWEEPS).astype(
        kappa.dtype
    )
    faces = face_table(kappa_ext)
    spatial_entries = thermal_offset
    state = excess_phonon_enthalpy
    fluxes = None
    for outer in range(OUTER):
        temp_slab = to_slab(spatial_entries)
        state, moments = kinetic(state, temp_slab, velocity, rates, capacity)
        reduced = sum_at_owner(moments, "mode", 3)
        summed = lax.all_to_all(reduced, "space", split_axis=2, concat_axis=1, tiled=True)
        blocks = jnp.transpose(summed, (0, 2, 3, 1))
        fluxes = blocks[1:]
        flux_ext = padded_2(
            fluxes.astype(jnp.bfloat16), (("space", 1), ("mode", 2)), SWEEPS
        ).astype(fluxes.dtype)
        rhs = -divergence(flux_ext)
        correction = chebyshev(rhs, faces, total, unchanged, matrix_height, matrix_breadth)
        spatial_entries = blocks[0] / total + correction
    return (spatial_entries, fluxes)


def solution(mesh):
    placed = (
        P("mode", "space", None, None),
        P("space", "mode", None),
        P("mode"),
        P("mode"),
        P("mode"),
        P("mode"),
        P(),
        P("space", "mode", None),
        P("space", "mode", None),
    )
    return jax.shard_map(
        per_device,
        mesh=mesh,
        in_specs=placed,
        out_specs=(P("space", "mode", None), P(None, "space", "mode", None)),
        check_vma=False,
    )
```

profile of v0, /device:TPU:31, one launch (start us, length us, event | category | flops | bytes accessed | tf_op | source)
XLA Modules:
  0.0 615.3 jit_solution(17676936092251280161)
XLA Ops:
  0.7 4.0 fusion.165
  11.0 6.4 %all-to-all-start = ((f32[8,1,1024]{2,1,0:T(1,128)}), f32[8,1,1024]{2,1,0:T(1,128)S(1)}, u32[]{:S(2)}, u32[]{:S(2)}) async-start(f32[8,1,1024]{2,1,0:T(1,128)} %reshape.250), calls=%async_computation | async-start | bytes 65536 | tf_op jit(solution)/shard_map/all_to_all | solution.py:180
  18.7 29.0 %all-to-all-done = f32[8,1,1024]{2,1,0:T(1,128)S(1)} async-done(((f32[8,1,1024]{2,1,0:T(1,128)}), f32[8,1,1024]{2,1,0:T(1,128)S(1)}, u32[]{:S(2)}, u32[]{:S(2)}) %all-to-all-start) | async-done | bytes 32800 | tf_op jit(solution)/shard_map/all_to_all | solution.py:180
  49.0 9.2 %all-to-all-start.3 = ((f32[16,1,1]{2,1,0:T(1,128)}), f32[16,1,1]{2,1,0:T(1,128)S(1)}, u32[]{:S(2)}, u32[]{:S(2)}) async-start(f32[16,1,1]{2,1,0:T(1,128)} %broadcast_in_dim.52), calls=%async_computation.3 | async-start | bytes 16384 | tf_op jit(solution)/shard_map/all_to_all | solution.py:34
  59.9 19.9 %all_gather.6 = f32[8,128,128]{1,2,0:T(8,128)S(1)} all-gather(f32[8,128,8]{1,2,0:T(8,128)S(1)} %all_to_all.65), channel_id=1, replica_groups=mesh['space'=8,'mode'=16] {'mode'}, dimensions={2}, use_global_device_ids=true | all-gather | bytes 557056 | tf_op jit(solution)/shard_map/all_gather | solution.py:181
  80.1 13.3 %pad_maximum_fusion = bf16[48,10,128,128]{3,2,1,0:T(8,128)(2,1)} fusion(bf16[48,1,128,128]{3,2,1,0:T(8,128)(2,1)} %collective-permute-done.1, bf16[48,8,128,128]{3,2,1,0:T(8,128)(2,1)} %param.13, bf16[48,1,128,128]{3,2,1,0:T(8,128)(2,1)} %collective-permute-done), kind=kLoop, calls=%fused_computation.96 | loop fusion | flops 15728640 | bytes 31457280 | tf_op jit(solution)/shard_map/concatenate | solution.py:21
  93.3 99.1 %while.28 = (s32[]{:T(128)}, f32[4,8,128,128]{3,0,2,1:T(4,128)S(1)}, bf16[6,8,8,128,128]{4,1,3,2,0:T(8,128)(2,1)}, f32[6,8]{1,0:T(8,128)S(1)}, f32[6,8]{1,0:T(8,...) while((s32[]{:T(128)}, ...), condition=%wide.region_2.3_spmd.clone, body=%wide.region_1.2_spmd.clone.sunk | while | flops 77856920 | bytes 49284748 | solution.py:206
  97.5 5.3 bitcast_dynamic-update-slice_fusion.2
  102.8 7.0 %select_add_fusion.4 = f32[4,8,128,128]{3,0,2,1:T(4,128)S(1)} fusion(f32[4,8,128,128]{3,0,2,1:T(4,128)S(1)} %get-tuple-element.704, f32[8,8,128,128]{3,0,2,1:T(8,128)} %get-tuple-element.671, pred[]{:T(512)S(6)} %compare.22, f32[1,8]{1,0:T(1,128)S(1)} %get-tuple-element.665, f32[1,8]{1,0:T(1,128)S(1)} %get-tuple-element.667, ...), kind=kOutput, calls=%fused_computation.20.clone.1 | convolution fusion | flops 51380320 | bytes 8388737 | tf_op jit(solution)/shard_map/while/body/eval_jaxpr/km,mzxy->kzxy/dot_general | solution.py:100
  114.0 5.3 bitcast_dynamic-update-slice_fusion.2
  119.4 7.0 %select_add_fusion.4 = f32[4,8,128,128]{3,0,2,1:T(4,128)S(1)} fusion(f32[4,8,128,128]{3,0,2,1:T(4,128)S(1)} %get-tuple-element.704, f32[8,8,128,128]{3,0,2,1:T(8,128)} %get-tuple-element.671, pred[]{:T(512)S(6)} %compare.22, f32[1,8]{1,0:T(1,128)S(1)} %get-tuple-element.665, f32[1,8]{1,0:T(1,128)S(1)} %get-tuple-element.667, ...), kind=kOutput, calls=%fused_computation.20.clone.1 | convolution fusion | flops 51380320 | bytes 8388737 | tf_op jit(solution)/shard_map/while/body/eval_jaxpr/km,mzxy->kzxy/dot_general | solution.py:100
  130.6 5.4 bitcast_dynamic-update-slice_fusion.2
  135.9 7.0 %select_add_fusion.4 = f32[4,8,128,128]{3,0,2,1:T(4,128)S(1)} fusion(f32[4,8,128,128]{3,0,2,1:T(4,128)S(1)} %get-tuple-element.704, f32[8,8,128,128]{3,0,2,1:T(8,128)} %get-tuple-element.671, pred[]{:T(512)S(6)} %compare.22, f32[1,8]{1,0:T(1,128)S(1)} %get-tuple-element.665, f32[1,8]{1,0:T(1,128)S(1)} %get-tuple-element.667, ...), kind=kOutput, calls=%fused_computation.20.clone.1 | convolution fusion | flops 51380320 | bytes 8388737 | tf_op jit(solution)/shard_map/while/body/eval_jaxpr/km,mzxy->kzxy/dot_general | solution.py:100
  147.1 5.3 bitcast_dynamic-update-slice_fusion.2
  152.4 7.0 %select_add_fusion.4 = f32[4,8,128,128]{3,0,2,1:T(4,128)S(1)} fusion(f32[4,8,128,128]{3,0,2,1:T(4,128)S(1)} %get-tuple-element.704, f32[8,8,128,128]{3,0,2,1:T(8,128)} %get-tuple-element.671, pred[]{:T(512)S(6)} %compare.22, f32[1,8]{1,0:T(1,128)S(1)} %get-tuple-element.665, f32[1,8]{1,0:T(1,128)S(1)} %get-tuple-element.667, ...), kind=kOutput, calls=%fused_computation.20.clone.1 | convolution fusion | flops 51380320 | bytes 8388737 | tf_op jit(solution)/shard_map/while/body/eval_jaxpr/km,mzxy->kzxy/dot_general | solution.py:100
  163.6 5.3 bitcast_dynamic-update-slice_fusion.2
  169.0 7.0 %select_add_fusion.4 = f32[4,8,128,128]{3,0,2,1:T(4,128)S(1)} fusion(f32[4,8,128,128]{3,0,2,1:T(4,128)S(1)} %get-tuple-element.704, f32[8,8,128,128]{3,0,2,1:T(8,128)} %get-tuple-element.671, pred[]{:T(512)S(6)} %compare.22, f32[1,8]{1,0:T(1,128)S(1)} %get-tuple-element.665, f32[1,8]{1,0:T(1,128)S(1)} %get-tuple-element.667, ...), kind=kOutput, calls=%fused_computation.20.clone.1 | convolution fusion | flops 51380320 | bytes 8388737 | tf_op jit(solution)/shard_map/while/body/eval_jaxpr/km,mzxy->kzxy/dot_general | solution.py:100
  180.2 5.3 bitcast_dynamic-update-slice_fusion.2
  185.4 7.0 %select_add_fusion.4 = f32[4,8,128,128]{3,0,2,1:T(4,128)S(1)} fusion(f32[4,8,128,128]{3,0,2,1:T(4,128)S(1)} %get-tuple-element.704, f32[8,8,128,128]{3,0,2,1:T(8,128)} %get-tuple-element.671, pred[]{:T(512)S(6)} %compare.22, f32[1,8]{1,0:T(1,128)S(1)} %get-tuple-element.665, f32[1,8]{1,0:T(1,128)S(1)} %get-tuple-element.667, ...), kind=kOutput, calls=%fused_computation.20.clone.1 | convolution fusion | flops 51380320 | bytes 8388737 | tf_op jit(solution)/shard_map/while/body/eval_jaxpr/km,mzxy->kzxy/dot_general | solution.py:100
  197.6 9.6 %all-to-all-start.1 = ((f32[16,4,8,128,8]{3,4,2,1,0:T(8,128)}), f32[16,4,8,128,8]{3,4,2,1,0:T(8,128)S(1)}, u32[]{:S(2)}, u32[]{:S(2)}) async-start(f32[16,4,8,128,8]{3,4,2,1,0:T(8,128)} %copy.139), calls=%async_computation.1 | async-start | bytes 4194304 | tf_op jit(solution)/shard_map/all_to_all | solution.py:49
  209.1 3.5 collective-permute-start.9
  214.0 7.4 %copy.135 = bf16[6,8,8,128,128]{4,3,2,1,0:T(8,128)(2,1)S(1)} copy(bf16[6,8,8,128,128]{4,1,3,2,0:T(8,128)(2,1)} %get-tuple-element.241) | data formatting | bytes 25165824 | tf_op jit(solution)/shard_map/while | solution.py:206
  223.4 4.0 collective-permute-start.2
  229.4 4.5 all-to-all-done.1
  237.6 3.9 all-to-all-start.2
  241.6 5.9 collective-permute-start.10
  249.4 18.8 %all-to-all-done.2 = f32[8,1,4096]{2,1,0:T(1,128)S(1)} async-done(((f32[8,1,4096]{2,1,0:T(1,128)}), f32[8,1,4096]{2,1,0:T(1,128)S(1)}, u32[]{:S(2)}, u32[]{:S(2)}) %all-to-all-start.2) | async-done | bytes 131104 | tf_op jit(solution)/shard_map/all_to_all | solution.py:243
  279.8 3.9 collective-permute-done.4
  284.0 3.8 collective-permute-done.5
  289.3 7.1 %collective-permute-start.6 = (bf16[3,24,4,64]{3,2,1,0:T(4,128)(2,1)S(1)}, bf16[3,24,4,64]{3,2,1,0:T(4,128)(2,1)S(1)}, u32[]{:S(2)}, u32[]{:S(2)}) collective-permute-start(bf16[3,24,4,64]{3,2,1,0:T(4,128)(2,1)S(1)} %get-tuple-element.528), channel_id=1, source_target_pairs={{0,1},{1,2},{2,3},{3,4},{4,5},{5,6},{6,7},{7,8},{8,9},{9,10},{10,1... | collective-permute-start | bytes 110600 | tf_op jit(solution)/shard_map/ppermute | solution.py:23
  301.5 3.6 copy.136
  305.1 3.6 copy.137
  320.5 3.9 all-to-all-start.4
  324.4 13.3 %pad_maximum_fusion.1 = bf16[6,8,10,128,128]{4,1,3,2,0:T(8,128)(2,1)} fusion(bf16[6,8,1,128,128]{4,1,3,2,0:T(8,128)(2,1)} %copy.137, bf16[6,8,8,128,128]{4,1,3,2,0:T(8,128)(2,1)} %get-tuple-element.241, bf16[6,8,1,128,128]{4,1,3,2,0:T(8,128)(2,1)} %copy.136), kind=kLoop, calls=%fused_computation.97 | loop fusion | flops 15728640 | bytes 31457280 | tf_op jit(solution)/shard_map/concatenate | solution.py:21
  340.5 24.7 %all_gather.7 = f32[8,128,128]{1,2,0:T(8,128)} all-gather(f32[8,128,8]{1,2,0:T(8,128)S(1)} %all_to_all.75), channel_id=1, replica_groups=mesh['space'=8,'mode'=16] {'mode'}, dimensions={2}, use_global_device_ids=true | all-gather | bytes 557056 | tf_op jit(solution)/shard_map/all_gather | solution.py:181
  367.3 136.7 %while.29 = (s32[]{:T(128)}, f32[4,8,128,128]{3,0,2,1:T(4,128)}, f32[6,8]{1,0:T(8,128)S(1)}, f32[6,8]{1,0:T(8,128)S(1)}, f32[6,8]{1,0:T(8,128)S(1)}, /*index=5*/...) while((s32[]{:T(128)}, f32[4,8,128,128]{3,0,2,1:T(4,128)}, ...), condition=%wide.region_7.8_spmd.clone, body=%wide.region_6.7_spmd.clone.sunk | while | flops 76808344 | bytes 54527136 | solution.py:206
  373.2 16.9 %select_add_fusion.5 = f32[4,8,128,128]{3,0,2,1:T(4,128)} fusion(f32[4,8,128,128]{3,0,2,1:T(4,128)} %get-tuple-element.739, f32[8,8,128,128]{3,0,2,1:T(8,128)} %slice.1269, f32[8,10,128,128]{3,0,2,1:T(8,128)} %copy-done, f32[8,128,128]{2,1,0:T(8,128)} %get-tuple-element.757, f32[8]{0:T(128)S(1)} %fusion.183, f32[8]{0:T(128)S(1)} %get-tuple-element.683, ...), kind=kOutput, calls=%fused_computation.62.clone.1 | convolution fusion | flops 75497568 | bytes 17301888 | tf_op jit(solution)/shard_map/while/body/eval_jaxpr/km,mzxy->kzxy/dot_general | solution.py:100
  396.0 16.9 %select_add_fusion.5 = f32[4,8,128,128]{3,0,2,1:T(4,128)} fusion(f32[4,8,128,128]{3,0,2,1:T(4,128)} %get-tuple-element.739, f32[8,8,128,128]{3,0,2,1:T(8,128)} %slice.1269, f32[8,10,128,128]{3,0,2,1:T(8,128)} %copy-done, f32[8,128,128]{2,1,0:T(8,128)} %get-tuple-element.757, f32[8]{0:T(128)S(1)} %fusion.183, f32[8]{0:T(128)S(1)} %get-tuple-element.683, ...), kind=kOutput, calls=%fused_computation.62.clone.1 | convolution fusion | flops 75497568 | bytes 17301888 | tf_op jit(solution)/shard_map/while/body/eval_jaxpr/km,mzxy->kzxy/dot_general | solution.py:100
  418.8 16.9 %select_add_fusion.5 = f32[4,8,128,128]{3,0,2,1:T(4,128)} fusion(f32[4,8,128,128]{3,0,2,1:T(4,128)} %get-tuple-element.739, f32[8,8,128,128]{3,0,2,1:T(8,128)} %slice.1269, f32[8,10,128,128]{3,0,2,1:T(8,128)} %copy-done, f32[8,128,128]{2,1,0:T(8,128)} %get-tuple-element.757, f32[8]{0:T(128)S(1)} %fusion.183, f32[8]{0:T(128)S(1)} %get-tuple-element.683, ...), kind=kOutput, calls=%fused_computation.62.clone.1 | convolution fusion | flops 75497568 | bytes 17301888 | tf_op jit(solution)/shard_map/while/body/eval_jaxpr/km,mzxy->kzxy/dot_general | solution.py:100
  441.5 16.9 %select_add_fusion.5 = f32[4,8,128,128]{3,0,2,1:T(4,128)} fusion(f32[4,8,128,128]{3,0,2,1:T(4,128)} %get-tuple-element.739, f32[8,8,128,128]{3,0,2,1:T(8,128)} %slice.1269, f32[8,10,128,128]{3,0,2,1:T(8,128)} %copy-done, f32[8,128,128]{2,1,0:T(8,128)} %get-tuple-element.757, f32[8]{0:T(128)S(1)} %fusion.183, f32[8]{0:T(128)S(1)} %get-tuple-element.683, ...), kind=kOutput, calls=%fused_computation.62.clone.1 | convolution fusion | flops 75497568 | bytes 17301888 | tf_op jit(solution)/shard_map/while/body/eval_jaxpr/km,mzxy->kzxy/dot_general | solution.py:100
  464.3 16.9 %select_add_fusion.5 = f32[4,8,128,128]{3,0,2,1:T(4,128)} fusion(f32[4,8,128,128]{3,0,2,1:T(4,128)} %get-tuple-element.739, f32[8,8,128,128]{3,0,2,1:T(8,128)} %slice.1269, f32[8,10,128,128]{3,0,2,1:T(8,128)} %copy-done, f32[8,128,128]{2,1,0:T(8,128)} %get-tuple-element.757, f32[8]{0:T(128)S(1)} %fusion.183, f32[8]{0:T(128)S(1)} %get-tuple-element.683, ...), kind=kOutput, calls=%fused_computation.62.clone.1 | convolution fusion | flops 75497568 | bytes 17301888 | tf_op jit(solution)/shard_map/while/body/eval_jaxpr/km,mzxy->kzxy/dot_general | solution.py:100
  487.1 16.9 %select_add_fusion.5 = f32[4,8,128,128]{3,0,2,1:T(4,128)} fusion(f32[4,8,128,128]{3,0,2,1:T(4,128)} %get-tuple-element.739, f32[8,8,128,128]{3,0,2,1:T(8,128)} %slice.1269, f32[8,10,128,128]{3,0,2,1:T(8,128)} %copy-done, f32[8,128,128]{2,1,0:T(8,128)} %get-tuple-element.757, f32[8]{0:T(128)S(1)} %fusion.183, f32[8]{0:T(128)S(1)} %get-tuple-element.683, ...), kind=kOutput, calls=%fused_computation.62.clone.1 | convolution fusion | flops 75497568 | bytes 17301888 | tf_op jit(solution)/shard_map/while/body/eval_jaxpr/km,mzxy->kzxy/dot_general | solution.py:100
  508.8 33.5 %all_to_all.88 = f32[16,4,8,128,8]{3,4,2,1,0:T(8,128)} all-to-all(f32[16,4,8,128,8]{3,4,2,1,0:T(8,128)S(1)} %copy.152), channel_id=1, replica_groups=mesh['space'=8,'mode'=16] {'mode'}, dimensions={0} | all-to-all | bytes 4194304 | tf_op jit(solution)/shard_map/all_to_all | solution.py:49
  549.5 8.2 %all_to_all.89 = f32[8,1,4096]{2,1,0:T(1,128)S(1)} all-to-all(f32[8,1,4096]{2,1,0:T(1,128)S(1)} %reshape.256), channel_id=1, replica_groups=mesh['space'=8,'mode'=16] {'space'}, dimensions={0} | all-to-all | bytes 262144 | tf_op jit(solution)/shard_map/all_to_all | solution.py:243
  566.8 3.5 collective-permute-start.12
  573.1 5.2 collective-permute-done.12
  579.7 4.0 collective-permute-done.13
  586.0 7.0 %collective-permute-start.14 = (bf16[3,24,4,64]{3,2,1,0:T(4,128)(2,1)S(1)}, bf16[3,24,4,64]{3,2,1,0:T(4,128)(2,1)S(1)}, u32[]{:S(2)}, u32[]{:S(2)}) collective-permute-start(bf16[3,24,4,64]{3,2,1,0:T(4,128)(2,1)S(1)} %get-tuple-element.526), channel_id=1, source_target_pairs={{0,1},{1,2},{2,3},{3,4},{4,5},{5,6},{6,7},{7,8},{8,9},{9,10},{10,1... | collective-permute-start | bytes 110600 | tf_op jit(solution)/shard_map/ppermute | solution.py:23
  (258 shorter events, 172.3 us)
Async XLA Ops:
  0.6 9.4 %copy-start.4 = (f32[16,8,64]{2,1,0:T(8,128)S(1)}, f32[16,8,64]{2,1,0:T(8,128)}, u32[]{:S(2)}) copy-start(f32[16,8,64]{2,1,0:T(8,128)} %param.14) | copy-start | bytes 98308
  0.6 16.8 %copy-start.11 = (s32[48]{0:T(128)S(1)}, s32[48]{0:T(128)}, u32[]{:S(2)}) copy-start(s32[48]{0:T(128)} %param.17) | copy-start | bytes 580
  0.7 16.8 %copy-start.10 = (f32[6]{0:T(128)S(1)}, f32[6]{0:T(128)}, u32[]{:S(2)}) copy-start(f32[6]{0:T(128)} %param.19) | copy-start | bytes 76
  0.7 16.9 %copy-start.7 = (s32[48]{0:T(128)S(1)}, s32[48]{0:T(128)}, u32[]{:S(2)}) copy-start(s32[48]{0:T(128)} %param.18) | copy-start | bytes 580
  0.7 17.0 %copy-start.8 = (f32[48]{0:T(128)S(1)}, f32[48]{0:T(128)}, u32[]{:S(2)}) copy-start(f32[48]{0:T(128)} %param.15) | copy-start | bytes 580
  0.7 17.0 %copy-start.9 = (f32[48]{0:T(128)S(1)}, f32[48]{0:T(128)}, u32[]{:S(2)}) copy-start(f32[48]{0:T(128)} %param.16) | copy-start | bytes 580
  4.7 75.4 %collective-permute-start = (bf16[48,1,128,128]{3,2,1,0:T(8,128)(2,1)}, bf16[48,1,128,128]{3,2,1,0:T(8,128)(2,1)}, u32[]{:S(2)}, u32[]{:S(2)}) collective-permute-start(bf16[48,1,128,128]{3,2,1,0:T(8,128)(2,1)} %get-tuple-element.508), channel_id=1, source_target_pairs={{0,16},{16,32},{32,48},{48,64},{64,80},{80,96},{96,112},{1,17},{17... | collective-permute-start | bytes 4718600 | tf_op jit(solution)/shard_map/ppermute | solution.py:23
  8.1 71.9 %collective-permute-start.1 = (bf16[48,1,128,128]{3,2,1,0:T(8,128)(2,1)}, bf16[48,1,128,128]{3,2,1,0:T(8,128)(2,1)}, u32[]{:S(2)}, u32[]{:S(2)}) collective-permute-start(bf16[48,1,128,128]{3,2,1,0:T(8,128)(2,1)} %get-tuple-element.509), channel_id=1, source_target_pairs={{16,0},{32,16},{48,32},{64,48},{80,64},{96,80},{112,96},{17,1},{33... | collective-permute-start | bytes 4718600 | tf_op jit(solution)/shard_map/ppermute | solution.py:25
  11.0 36.7 %all-to-all-start = ((f32[8,1,1024]{2,1,0:T(1,128)}), f32[8,1,1024]{2,1,0:T(1,128)S(1)}, u32[]{:S(2)}, u32[]{:S(2)}) async-start(f32[8,1,1024]{2,1,0:T(1,128)} %reshape.250), calls=%async_computation | async-start | bytes 65536 | tf_op jit(solution)/shard_map/all_to_all | solution.py:180
  49.0 148.6 %all-to-all-start.3 = ((f32[16,1,1]{2,1,0:T(1,128)}), f32[16,1,1]{2,1,0:T(1,128)S(1)}, u32[]{:S(2)}, u32[]{:S(2)}) async-start(f32[16,1,1]{2,1,0:T(1,128)} %broadcast_in_dim.52), calls=%async_computation.3 | async-start | bytes 16384 | tf_op jit(solution)/shard_map/all_to_all | solution.py:34
  194.3 12.9 %copy-start.5 = (f32[16,8,64]{2,1,0:T(8,128)S(1)}, f32[16,8,64]{2,1,0:T(8,128)}, u32[]{:S(2)}) copy-start(f32[16,8,64]{2,1,0:T(8,128)} %param.20) | copy-start | bytes 98308
  194.3 12.9 %copy-start.6 = (s32[16,8,64]{2,1,0:T(8,128)S(1)}, s32[16,8,64]{2,1,0:T(8,128)}, u32[]{:S(2)}) copy-start(s32[16,8,64]{2,1,0:T(8,128)} %param.21) | copy-start | bytes 98308
  197.6 36.4 %all-to-all-start.1 = ((f32[16,4,8,128,8]{3,4,2,1,0:T(8,128)}), f32[16,4,8,128,8]{3,4,2,1,0:T(8,128)S(1)}, u32[]{:S(2)}, u32[]{:S(2)}) async-start(f32[16,4,8,128,8]{3,4,2,1,0:T(8,128)} %copy.139), calls=%async_computation.1 | async-start | bytes 4194304 | tf_op jit(solution)/shard_map/all_to_all | solution.py:49
  207.2 22.2 %collective-permute-start.8 = (bf16[4,8,64]{2,1,0:T(8,128)(2,1)S(1)}, bf16[4,8,64]{2,1,0:T(8,128)(2,1)S(1)}, u32[]{:S(2)}, u32[]{:S(2)}) collective-permute-start(bf16[4,8,64]{2,1,0:T(8,128)(2,1)S(1)} %get-tuple-element.532), channel_id=1, source_target_pairs={{0,16},{16,32},{32,48},{48,64},{64,80},{80,96},{96,112},{1,17},{17... | collective-permute-start | bytes 12296 | tf_op jit(solution)/shard_map/ppermute | solution.py:23
  209.1 20.3 %collective-permute-start.9 = (bf16[4,8,64]{2,1,0:T(8,128)(2,1)S(1)}, bf16[4,8,64]{2,1,0:T(8,128)(2,1)S(1)}, u32[]{:S(2)}, u32[]{:S(2)}) collective-permute-start(bf16[4,8,64]{2,1,0:T(8,128)(2,1)S(1)} %get-tuple-element.533), channel_id=1, source_target_pairs={{16,0},{32,16},{48,32},{64,48},{80,64},{96,80},{112,96},{17,1},{33... | collective-permute-start | bytes 12296 | tf_op jit(solution)/shard_map/ppermute | solution.py:25
  223.4 78.0 %collective-permute-start.2 = (bf16[48,1,128,128]{3,2,1,0:T(8,128)(2,1)}, bf16[48,1,128,128]{3,2,1,0:T(8,128)(2,1)}, u32[]{:S(2)}, u32[]{:S(2)}) collective-permute-start(bf16[48,1,128,128]{3,2,1,0:T(8,128)(2,1)} %get-tuple-element.506), channel_id=1, source_target_pairs={{0,16},{16,32},{32,48},{48,64},{64,80},{80,96},{96,112},{1,17},{17... | collective-permute-start | bytes 4718600 | tf_op jit(solution)/shard_map/ppermute | solution.py:23
  227.5 77.6 %collective-permute-start.3 = (bf16[48,1,128,128]{3,2,1,0:T(8,128)(2,1)}, bf16[48,1,128,128]{3,2,1,0:T(8,128)(2,1)}, u32[]{:S(2)}, u32[]{:S(2)}) collective-permute-start(bf16[48,1,128,128]{3,2,1,0:T(8,128)(2,1)} %get-tuple-element.507), channel_id=1, source_target_pairs={{16,0},{32,16},{48,32},{64,48},{80,64},{96,80},{112,96},{17,1},{33... | collective-permute-start | bytes 4718600 | tf_op jit(solution)/shard_map/ppermute | solution.py:25
  237.6 30.6 %all-to-all-start.2 = ((f32[8,1,4096]{2,1,0:T(1,128)}), f32[8,1,4096]{2,1,0:T(1,128)S(1)}, u32[]{:S(2)}, u32[]{:S(2)}) async-start(f32[8,1,4096]{2,1,0:T(1,128)} %reshape.252), calls=%async_computation.2 | async-start | bytes 262144 | tf_op jit(solution)/shard_map/all_to_all | solution.py:243
  241.6 33.1 %collective-permute-start.10 = (bf16[24,4,64]{2,1,0:T(4,128)(2,1)S(1)}, bf16[24,4,64]{2,1,0:T(4,128)(2,1)S(1)}, u32[]{:S(2)}, u32[]{:S(2)}) collective-permute-start(bf16[24,4,64]{2,1,0:T(4,128)(2,1)S(1)} %get-tuple-element.530), channel_id=1, source_target_pairs={{0,1},{1,2},{2,3},{3,4},{4,5},{5,6},{6,7},{7,8},{8,9},{9,10},{10,1... | collective-permute-start | bytes 36872 | tf_op jit(solution)/shard_map/ppermute | solution.py:23
  247.5 30.6 %collective-permute-start.11 = (bf16[24,4,64]{2,1,0:T(4,128)(2,1)S(1)}, bf16[24,4,64]{2,1,0:T(4,128)(2,1)S(1)}, u32[]{:S(2)}, u32[]{:S(2)}) collective-permute-start(bf16[24,4,64]{2,1,0:T(4,128)(2,1)S(1)} %get-tuple-element.531), channel_id=1, source_target_pairs={{1,0},{2,1},{3,2},{4,3},{5,4},{6,5},{7,6},{8,7},{9,8},{10,9},{11,1... | collective-permute-start | bytes 36872 | tf_op jit(solution)/shard_map/ppermute | solution.py:25
  271.5 24.8 %copy-start.2 = (f32[4,8,8,16,8]{3,4,2,1,0:T(8,128)}, f32[4,8,8,16,8]{3,4,2,1,0:T(8,128)S(1)}, u32[]{:S(2)}) copy-start(f32[4,8,8,16,8]{3,4,2,1,0:T(8,128)S(1)} %copy.142) | copy-start | bytes 393220
  272.8 10.9 %collective-permute-start.4 = (bf16[3,4,8,64]{1,2,3,0:T(8,128)(2,1)}, bf16[3,4,8,64]{1,2,3,0:T(8,128)(2,1)S(1)}, u32[]{:S(2)}, u32[]{:S(2)}) collective-permute-start(bf16[3,4,8,64]{1,2,3,0:T(8,128)(2,1)} %get-tuple-element.522), channel_id=1, source_target_pairs={{0,16},{16,32},{32,48},{48,64},{64,80},{80,96},{96,112},{1,17},{17... | collective-permute-start | bytes 36872 | tf_op jit(solution)/shard_map/ppermute | solution.py:23
  274.7 13.1 %collective-permute-start.5 = (bf16[3,4,8,64]{1,2,3,0:T(8,128)(2,1)}, bf16[3,4,8,64]{1,2,3,0:T(8,128)(2,1)}, u32[]{:S(2)}, u32[]{:S(2)}) collective-permute-start(bf16[3,4,8,64]{1,2,3,0:T(8,128)(2,1)} %get-tuple-element.523), channel_id=1, source_target_pairs={{16,0},{32,16},{48,32},{64,48},{80,64},{96,80},{112,96},{17,1},{33... | collective-permute-start | bytes 36872 | tf_op jit(solution)/shard_map/ppermute | solution.py:25
  289.3 19.4 %collective-permute-start.6 = (bf16[3,24,4,64]{3,2,1,0:T(4,128)(2,1)S(1)}, bf16[3,24,4,64]{3,2,1,0:T(4,128)(2,1)S(1)}, u32[]{:S(2)}, u32[]{:S(2)}) collective-permute-start(bf16[3,24,4,64]{3,2,1,0:T(4,128)(2,1)S(1)} %get-tuple-element.528), channel_id=1, source_target_pairs={{0,1},{1,2},{2,3},{3,4},{4,5},{5,6},{6,7},{7,8},{8,9},{9,10},{10,1... | collective-permute-start | bytes 110600 | tf_op jit(solution)/shard_map/ppermute | solution.py:23
  296.3 12.3 %collective-permute-start.7 = (bf16[3,24,4,64]{3,2,1,0:T(4,128)(2,1)S(1)}, bf16[3,24,4,64]{3,2,1,0:T(4,128)(2,1)S(1)}, u32[]{:S(2)}, u32[]{:S(2)}) collective-permute-start(bf16[3,24,4,64]{3,2,1,0:T(4,128)(2,1)S(1)} %get-tuple-element.529), channel_id=1, source_target_pairs={{1,0},{2,1},{3,2},{4,3},{5,4},{6,5},{7,6},{8,7},{9,8},{10,9},{11,1... | collective-permute-start | bytes 110600 | tf_op jit(solution)/shard_map/ppermute | solution.py:25
  311.7 1.0 copy-start.1
  320.5 17.3 %all-to-all-start.4 = ((f32[8,1,1024]{2,1,0:T(1,128)}), f32[8,1,1024]{2,1,0:T(1,128)S(1)}, u32[]{:S(2)}, u32[]{:S(2)}) async-start(f32[8,1,1024]{2,1,0:T(1,128)} %reshape.254), calls=%async_computation.4 | async-start | bytes 65536 | tf_op jit(solution)/shard_map/all_to_all | solution.py:180
  369.5 3.7 copy-start
  392.3 3.7 copy-start
  415.1 3.7 copy-start
  437.9 3.7 copy-start
  460.7 3.7 copy-start
  483.4 3.7 copy-start
  566.8 11.6 %collective-permute-start.12 = (bf16[3,4,8,64]{1,2,3,0:T(8,128)(2,1)}, bf16[3,4,8,64]{1,2,3,0:T(8,128)(2,1)}, u32[]{:S(2)}, u32[]{:S(2)}) collective-permute-start(bf16[3,4,8,64]{1,2,3,0:T(8,128)(2,1)} %get-tuple-element.524), channel_id=1, source_target_pairs={{0,16},{16,32},{32,48},{48,64},{64,80},{80,96},{96,112},{1,17},{17... | collective-permute-start | bytes 36872 | tf_op jit(solution)/shard_map/ppermute | solution.py:23
  570.3 13.3 %collective-permute-start.13 = (bf16[3,4,8,64]{1,2,3,0:T(8,128)(2,1)}, bf16[3,4,8,64]{1,2,3,0:T(8,128)(2,1)}, u32[]{:S(2)}, u32[]{:S(2)}) collective-permute-start(bf16[3,4,8,64]{1,2,3,0:T(8,128)(2,1)} %get-tuple-element.525), channel_id=1, source_target_pairs={{16,0},{32,16},{48,32},{64,48},{80,64},{96,80},{112,96},{17,1},{33... | collective-permute-start | bytes 36872 | tf_op jit(solution)/shard_map/ppermute | solution.py:25
  586.0 13.2 %collective-permute-start.14 = (bf16[3,24,4,64]{3,2,1,0:T(4,128)(2,1)S(1)}, bf16[3,24,4,64]{3,2,1,0:T(4,128)(2,1)S(1)}, u32[]{:S(2)}, u32[]{:S(2)}) collective-permute-start(bf16[3,24,4,64]{3,2,1,0:T(4,128)(2,1)S(1)} %get-tuple-element.526), channel_id=1, source_target_pairs={{0,1},{1,2},{2,3},{3,4},{4,5},{5,6},{6,7},{7,8},{8,9},{9,10},{10,1... | collective-permute-start | bytes 110600 | tf_op jit(solution)/shard_map/ppermute | solution.py:23
  592.9 9.4 %collective-permute-start.15 = (bf16[3,24,4,64]{3,2,1,0:T(4,128)(2,1)S(1)}, bf16[3,24,4,64]{3,2,1,0:T(4,128)(2,1)}, u32[]{:S(2)}, u32[]{:S(2)}) collective-permute-start(bf16[3,24,4,64]{3,2,1,0:T(4,128)(2,1)S(1)} %get-tuple-element.527), channel_id=1, source_target_pairs={{1,0},{2,1},{3,2},{4,3},{5,4},{6,5},{7,6},{8,7},{9,8},{10,9},{11,1... | collective-permute-start | bytes 110600 | tf_op jit(solution)/shard_map/ppermute | solution.py:25
  599.2 0.6 copy-start.3
where the time goes:
time: 626 us; the launch traced here: 615 us
  matrix products  143 us (23%)
  local copies, waits for them, and re-layouts  113 us (18%)
  other arithmetic  111 us (18%)
  starting transfers between devices  86.7 us (14%)
  blocking collectives  86.3 us (14%)
  waiting for transfers between devices  71.9 us (11%)
    dot_general x12, matrix products, upwind(): jnp.einsum('km,mzxy->kzxy', weights, updated, precision=lax.Precision.HIG...  143 us
    all_gather x2, blocking collectives, to_slab(): return lax.all_gather(moved, 'mode', axis=2, tiled=True)  44.6 us
    ppermute x8, starting transfers between devices, padded_2(): lax.ppermute(tail, axis, [(i, (i + 1) % count) for i in range(ends)])  34.7 us
    all_to_all x1, blocking collectives, sum_at_owner(): lax.all_to_all(in_blocks(shard, dim, length), axis, 0, 0, tiled=True)  33.5 us
    dynamic_update_slice x6, other arithmetic, kinetic(): moments, news = lax.scan(step, start, (shaped,) + params)  31.9 us
    all_to_all x2, waiting for transfers between devices, to_slab(): lax.all_to_all(upright, 'space', split_axis=0, concat_axis=1, tiled=True)  29 us
    concatenate x8, other arithmetic, padded_2(): jnp.concatenate([lax.ppermute(tail, axis, [(i, (i + 1) % count) for i in...  29 us
    convert_element_type x12, other arithmetic, step(): block.astype(jnp.float32)  23.6 us
  transfers between devices with their start and end apart: 21, of which 8 were waited for; matrix products, arithmetic and copies ran while one was open for 28% of the time, Pallas kernels for 0%

commit v1 on v0

--- a/solution.py
+++ b/solution.py
@@ -10,6 +10,13 @@
 time_step = 0.25
 pore_factor = 0.1
 kappa_top = 1.0
+
+
+def gather_over(array, mesh_axis, dim):
+    devices = lax.axis_size(mesh_axis)
+    pieces = jnp.stack([array for _ in range(devices)])
+    pieces = lax.all_to_all(pieces, mesh_axis, split_axis=0, concat_axis=0)
+    return jnp.concatenate(pieces, axis=dim)
 
 
 def padded_2(cells, sides, width):
@@ -178,7 +185,7 @@
 def to_slab(block):
     upright = jnp.transpose(block, (2, 0, 1))
     moved = lax.all_to_all(upright, "space", split_axis=0, concat_axis=1, tiled=True)
-    return lax.all_gather(moved, "mode", axis=2, tiled=True)
+    return gather_over(moved, "mode", 2)
 
 
 def kinetic(state, temp_slab, velocity, rates, capacity):

time: 626 us -> 693 us (1.11)
  other arithmetic: 111 us -> 163 us
  blocking collectives: 86.3 us -> 41.6 us
  local copies, waits for them, and re-layouts: 113 us -> 149 us
  waiting for transfers between devices: 71.9 us -> 83.8 us
  starting transfers between devices: 86.7 us -> 98.1 us
    dynamic_update_slice x6, other arithmetic: 31.9 us -> 84.3 us  [kinetic(): moments, news = lax.scan(step, start, (shaped,) + params)]
    all_gather x2 -> x0, blocking collectives: 44.6 us -> none  [to_slab(): return lax.all_gather(moved, 'mode', axis=2, tiled=True)]
    all_to_all x1, waiting for transfers between devices: 18.8 us -> 2.6 us  [per_device(): lax.all_to_all(reduced, 'space', split_axis=2, concat_axis=1, tiled=True)]
    all_to_all x0 -> x2, starting transfers between devices: none -> 15.4 us  [gather_over(): pieces = lax.all_to_all(pieces, mesh_axis, split_axis=0, concat_axis=0)]
    slice x12, local copies, waits for them, and re-layouts: 16.5 us -> 30.1 us  [upwind(): current = padded[:, 1:-1]]
    mul x12 -> x24, local copies, waits for them, and re-layouts: 0.09 us -> 11.5 us  [upwind(): widen(capacity) * temp_slab[None] - current]
    ppermute x8, waiting for transfers between devices: 9.12 us -> 20.5 us  [padded_2(): lax.ppermute(tail, axis, [(i, (i + 1) % count) for i in range(ends)])]
    all_to_all x0 -> x2, waiting for transfers between devices: none -> 8.88 us  [gather_over(): pieces = lax.all_to_all(pieces, mesh_axis, split_axis=0, concat_axis=0)]
  transfers between devices with their start and end apart: 21 -> 23, of which waited for: 8 -> 10; matrix products, arithmetic and copies ran while one was open for 28% -> 37% of each run, Pallas kernels for 0% -> 0%
where the time goes in v1:
time: 693 us; the launch traced here: 681 us
  other arithmetic  163 us (24%)
  local copies, waits for them, and re-layouts  149 us (22%)
  matrix products  142 us (20%)
  starting transfers between devices  98.1 us (14%)
  waiting for transfers between devices  83.8 us (12%)
  blocking collectives  41.6 us (6%)
    dot_general x12, matrix products, upwind(): jnp.einsum('km,mzxy->kzxy', weights, updated, precision=lax.Precision.HIG...  142 us
    dynamic_update_slice x6, other arithmetic, kinetic(): moments, news = lax.scan(step, start, (shaped,) + params)  84.3 us
    ppermute x8, starting transfers between devices, padded_2(): lax.ppermute(tail, axis, [(i, (i + 1) % count) for i in range(ends)])  36.8 us
    all_to_all x1, blocking collectives, sum_at_owner(): lax.all_to_all(in_blocks(shard, dim, length), axis, 0, 0, tiled=True)  34 us
    all_to_all x2, waiting for transfers between devices, to_slab(): lax.all_to_all(upright, 'space', split_axis=0, concat_axis=1, tiled=True)  30.1 us
    slice x12, local copies, waits for them, and re-layouts, upwind(): current = padded[:, 1:-1]  30.1 us
    concatenate x8, other arithmetic, padded_2(): jnp.concatenate([lax.ppermute(tail, axis, [(i, (i + 1) % count) for i in...  27.1 us
    convert_element_type x12, other arithmetic, step(): block.astype(jnp.float32)  23.6 us
  transfers between devices with their start and end apart: 23, of which 10 were waited for; matrix products, arithmetic and copies ran while one was open for 37% of the time, Pallas kernels for 0%

profile of v1, /device:TPU:31, one launch (start us, length us, event | category | flops | bytes accessed | tf_op | source)
XLA Modules:
  0.0 680.6 jit_solution(744312604416130340)
XLA Ops:
  0.7 4.0 fusion.165
  11.0 6.4 all-to-all-start
  17.6 30.1 %all-to-all-done = f32[8,1,1024]{2,1,0:T(1,128)S(1)} async-done(((f32[8,1,1024]{2,1,0:T(1,128)}), f32[8,1,1024]{2,1,0:T(1,128)S(1)}, u32[]{:S(2)}, u32[]{:S(2)}) %all-to-all-start) | async-done | bytes 32800 | tf_op jit(solution)/shard_map/all_to_all | solution.py:187
  50.3 9.2 %all-to-all-start.1 = ((f32[16,8,128,8]{2,3,1,0:T(8,128)}), f32[16,8,128,8]{2,3,1,0:T(8,128)S(1)}, u32[]{:S(2)}, u32[]{:S(2)}) async-start(f32[16,8,128,8]{2,3,1,0:T(8,128)} %stack.19), calls=%async_computation.1 | async-start | bytes 1048576 | tf_op jit(solution)/shard_map/all_to_all | solution.py:18
  60.6 8.9 %all-to-all-done.1 = f32[16,8,128,8]{2,3,1,0:T(8,128)S(1)} async-done(((f32[16,8,128,8]{2,3,1,0:T(8,128)}), f32[16,8,128,8]{2,3,1,0:T(8,128)S(1)}, u32[]{:S(2)}, u32[]{:S(2)}) %all-to-all-start.1) | async-done | bytes 524320 | tf_op jit(solution)/shard_map/all_to_all | solution.py:18
  70.8 5.7 all-to-all-start.4
  76.5 13.3 %pad_maximum_fusion = bf16[48,10,128,128]{3,2,1,0:T(8,128)(2,1)} fusion(bf16[48,1,128,128]{3,2,1,0:T(8,128)(2,1)} %collective-permute-done.1, bf16[48,8,128,128]{3,2,1,0:T(8,128)(2,1)} %param.13, bf16[48,1,128,128]{3,2,1,0:T(8,128)(2,1)} %collective-permute-done), kind=kLoop, calls=%fused_computation.96 | loop fusion | flops 15728640 | bytes 31457280 | tf_op jit(solution)/shard_map/concatenate | solution.py:28
  89.8 172.2 %while.28 = (s32[]{:T(128)}, f32[4,8,128,128]{3,0,2,1:T(4,128)S(1)}, bf16[6,8,8,128,128]{4,1,3,2,0:T(8,128)(2,1)}, f32[6,8]{1,0:T(8,128)S(1)}, f32[6,8]{1,0:T(8,...) while((s32[]{:T(128)}, ...), condition=%wide.region_2.3_spmd.clone, body=%wide.region_1.2_spmd.clone.sunk | while | flops 77856920 | bytes 71304872 | solution.py:213
  97.5 14.0 %bitcast_dynamic-update-slice_fusion.2 = (bf16[6,8,8,128,128]{4,1,3,2,0:T(8,128)(2,1)}, f32[8,8,128,128]{3,0,2,1:T(8,128)}) fusion(bf16[6,8,8,128,128]{4,1,3,2,0:T(8,128)(2,1)} %get-tuple-element.696, s32[]{:T(128)} %get-tuple-element.694, f32[8,8,128,128]{3,0,2,1:T(8,128)} %slice.1262, f32[8,128,128]{2,1,0:T(8,128)S(1)} %copy.187, ...), kind=kLoop, calls=%fused_computation.19.clone.1 | loop fusion | flops 25165824 | bytes 19399424 | tf_op jit(solution)/shard_map/while/body/jit(dynamic_update_index_in_dim)/dynamic_update_slice | solution.py:213
  111.5 7.0 %select_add_fusion.4 = f32[4,8,128,128]{3,0,2,1:T(4,128)S(1)} fusion(f32[4,8,128,128]{3,0,2,1:T(4,128)S(1)} %get-tuple-element.695, f32[8,8,128,128]{3,0,2,1:T(8,128)} %get-tuple-element.662, pred[]{:T(512)S(6)} %compare.22, f32[1,8]{1,0:T(1,128)S(1)} %get-tuple-element.656, f32[1,8]{1,0:T(1,128)S(1)} %get-tuple-element.658, ...), kind=kOutput, calls=%fused_computation.20.clone.1 | convolution fusion | flops 51380320 | bytes 8388737 | tf_op jit(solution)/shard_map/while/body/eval_jaxpr/km,mzxy->kzxy/dot_general | solution.py:107
  126.2 14.0 %bitcast_dynamic-update-slice_fusion.2 = (bf16[6,8,8,128,128]{4,1,3,2,0:T(8,128)(2,1)}, f32[8,8,128,128]{3,0,2,1:T(8,128)}) fusion(bf16[6,8,8,128,128]{4,1,3,2,0:T(8,128)(2,1)} %get-tuple-element.696, s32[]{:T(128)} %get-tuple-element.694, f32[8,8,128,128]{3,0,2,1:T(8,128)} %slice.1262, f32[8,128,128]{2,1,0:T(8,128)S(1)} %copy.187, ...), kind=kLoop, calls=%fused_computation.19.clone.1 | loop fusion | flops 25165824 | bytes 19399424 | tf_op jit(solution)/shard_map/while/body/jit(dynamic_update_index_in_dim)/dynamic_update_slice | solution.py:213
  140.2 7.0 %select_add_fusion.4 = f32[4,8,128,128]{3,0,2,1:T(4,128)S(1)} fusion(f32[4,8,128,128]{3,0,2,1:T(4,128)S(1)} %get-tuple-element.695, f32[8,8,128,128]{3,0,2,1:T(8,128)} %get-tuple-element.662, pred[]{:T(512)S(6)} %compare.22, f32[1,8]{1,0:T(1,128)S(1)} %get-tuple-element.656, f32[1,8]{1,0:T(1,128)S(1)} %get-tuple-element.658, ...), kind=kOutput, calls=%fused_computation.20.clone.1 | convolution fusion | flops 51380320 | bytes 8388737 | tf_op jit(solution)/shard_map/while/body/eval_jaxpr/km,mzxy->kzxy/dot_general | solution.py:107
  154.9 14.1 %bitcast_dynamic-update-slice_fusion.2 = (bf16[6,8,8,128,128]{4,1,3,2,0:T(8,128)(2,1)}, f32[8,8,128,128]{3,0,2,1:T(8,128)}) fusion(bf16[6,8,8,128,128]{4,1,3,2,0:T(8,128)(2,1)} %get-tuple-element.696, s32[]{:T(128)} %get-tuple-element.694, f32[8,8,128,128]{3,0,2,1:T(8,128)} %slice.1262, f32[8,128,128]{2,1,0:T(8,128)S(1)} %copy.187, ...), kind=kLoop, calls=%fused_computation.19.clone.1 | loop fusion | flops 25165824 | bytes 19399424 | tf_op jit(solution)/shard_map/while/body/jit(dynamic_update_index_in_dim)/dynamic_update_slice | solution.py:213
  168.9 7.0 %select_add_fusion.4 = f32[4,8,128,128]{3,0,2,1:T(4,128)S(1)} fusion(f32[4,8,128,128]{3,0,2,1:T(4,128)S(1)} %get-tuple-element.695, f32[8,8,128,128]{3,0,2,1:T(8,128)} %get-tuple-element.662, pred[]{:T(512)S(6)} %compare.22, f32[1,8]{1,0:T(1,128)S(1)} %get-tuple-element.656, f32[1,8]{1,0:T(1,128)S(1)} %get-tuple-element.658, ...), kind=kOutput, calls=%fused_computation.20.clone.1 | convolution fusion | flops 51380320 | bytes 8388737 | tf_op jit(solution)/shard_map/while/body/eval_jaxpr/km,mzxy->kzxy/dot_general | solution.py:107
  183.6 14.0 %bitcast_dynamic-update-slice_fusion.2 = (bf16[6,8,8,128,128]{4,1,3,2,0:T(8,128)(2,1)}, f32[8,8,128,128]{3,0,2,1:T(8,128)}) fusion(bf16[6,8,8,128,128]{4,1,3,2,0:T(8,128)(2,1)} %get-tuple-element.696, s32[]{:T(128)} %get-tuple-element.694, f32[8,8,128,128]{3,0,2,1:T(8,128)} %slice.1262, f32[8,128,128]{2,1,0:T(8,128)S(1)} %copy.187, ...), kind=kLoop, calls=%fused_computation.19.clone.1 | loop fusion | flops 25165824 | bytes 19399424 | tf_op jit(solution)/shard_map/while/body/jit(dynamic_update_index_in_dim)/dynamic_update_slice | solution.py:213
  197.6 7.0 %select_add_fusion.4 = f32[4,8,128,128]{3,0,2,1:T(4,128)S(1)} fusion(f32[4,8,128,128]{3,0,2,1:T(4,128)S(1)} %get-tuple-element.695, f32[8,8,128,128]{3,0,2,1:T(8,128)} %get-tuple-element.662, pred[]{:T(512)S(6)} %compare.22, f32[1,8]{1,0:T(1,128)S(1)} %get-tuple-element.656, f32[1,8]{1,0:T(1,128)S(1)} %get-tuple-element.658, ...), kind=kOutput, calls=%fused_computation.20.clone.1 | convolution fusion | flops 51380320 | bytes 8388737 | tf_op jit(solution)/shard_map/while/body/eval_jaxpr/km,mzxy->kzxy/dot_general | solution.py:107
  212.3 14.0 %bitcast_dynamic-update-slice_fusion.2 = (bf16[6,8,8,128,128]{4,1,3,2,0:T(8,128)(2,1)}, f32[8,8,128,128]{3,0,2,1:T(8,128)}) fusion(bf16[6,8,8,128,128]{4,1,3,2,0:T(8,128)(2,1)} %get-tuple-element.696, s32[]{:T(128)} %get-tuple-element.694, f32[8,8,128,128]{3,0,2,1:T(8,128)} %slice.1262, f32[8,128,128]{2,1,0:T(8,128)S(1)} %copy.187, ...), kind=kLoop, calls=%fused_computation.19.clone.1 | loop fusion | flops 25165824 | bytes 19399424 | tf_op jit(solution)/shard_map/while/body/jit(dynamic_update_index_in_dim)/dynamic_update_slice | solution.py:213
  226.3 7.0 %select_add_fusion.4 = f32[4,8,128,128]{3,0,2,1:T(4,128)S(1)} fusion(f32[4,8,128,128]{3,0,2,1:T(4,128)S(1)} %get-tuple-element.695, f32[8,8,128,128]{3,0,2,1:T(8,128)} %get-tuple-element.662, pred[]{:T(512)S(6)} %compare.22, f32[1,8]{1,0:T(1,128)S(1)} %get-tuple-element.656, f32[1,8]{1,0:T(1,128)S(1)} %get-tuple-element.658, ...), kind=kOutput, calls=%fused_computation.20.clone.1 | convolution fusion | flops 51380320 | bytes 8388737 | tf_op jit(solution)/shard_map/while/body/eval_jaxpr/km,mzxy->kzxy/dot_general | solution.py:107
  241.0 14.1 %bitcast_dynamic-update-slice_fusion.2 = (bf16[6,8,8,128,128]{4,1,3,2,0:T(8,128)(2,1)}, f32[8,8,128,128]{3,0,2,1:T(8,128)}) fusion(bf16[6,8,8,128,128]{4,1,3,2,0:T(8,128)(2,1)} %get-tuple-element.696, s32[]{:T(128)} %get-tuple-element.694, f32[8,8,128,128]{3,0,2,1:T(8,128)} %slice.1262, f32[8,128,128]{2,1,0:T(8,128)S(1)} %copy.187, ...), kind=kLoop, calls=%fused_computation.19.clone.1 | loop fusion | flops 25165824 | bytes 19399424 | tf_op jit(solution)/shard_map/while/body/jit(dynamic_update_index_in_dim)/dynamic_update_slice | solution.py:213
  255.1 7.0 %select_add_fusion.4 = f32[4,8,128,128]{3,0,2,1:T(4,128)S(1)} fusion(f32[4,8,128,128]{3,0,2,1:T(4,128)S(1)} %get-tuple-element.695, f32[8,8,128,128]{3,0,2,1:T(8,128)} %get-tuple-element.662, pred[]{:T(512)S(6)} %compare.22, f32[1,8]{1,0:T(1,128)S(1)} %get-tuple-element.656, f32[1,8]{1,0:T(1,128)S(1)} %get-tuple-element.658, ...), kind=kOutput, calls=%fused_computation.20.clone.1 | convolution fusion | flops 51380320 | bytes 8388737 | tf_op jit(solution)/shard_map/while/body/eval_jaxpr/km,mzxy->kzxy/dot_general | solution.py:107
  267.2 7.3 %all-to-all-start.2 = ((f32[16,4,8,128,8]{3,4,2,1,0:T(8,128)}), f32[16,4,8,128,8]{3,4,2,1,0:T(8,128)S(1)}, u32[]{:S(2)}, u32[]{:S(2)}) async-start(f32[16,4,8,128,8]{3,4,2,1,0:T(8,128)} %copy.149), calls=%async_computation.2 | async-start | bytes 4194304 | tf_op jit(solution)/shard_map/all_to_all | solution.py:56
  279.8 3.8 collective-permute-done.9
  283.7 5.8 collective-permute-start.10
  293.0 8.2 %all-to-all-done.2 = f32[16,4,8,128,8]{3,4,2,1,0:T(8,128)S(1)} async-done(((f32[16,4,8,128,8]{3,4,2,1,0:T(8,128)}), f32[16,4,8,128,8]{3,4,2,1,0:T(8,128)S(1)}, u32[]{:S(2)}, u32[]{:S(2)}) %all-to-all-start.2) | async-done | bytes 2097184 | tf_op jit(solution)/shard_map/all_to_all | solution.py:56
  304.9 3.9 all-to-all-start.3
  327.9 11.5 %copy.145 = bf16[6,8,8,128,128]{4,3,2,1,0:T(8,128)(2,1)} copy(bf16[6,8,8,128,128]{4,1,3,2,0:T(8,128)(2,1)} %get-tuple-element.241) | data formatting | bytes 25165824 | tf_op jit(solution)/shard_map/while | solution.py:213
  341.5 7.3 %collective-permute-start.6 = (bf16[3,24,4,64]{3,2,1,0:T(4,128)(2,1)S(1)}, bf16[3,24,4,64]{3,2,1,0:T(4,128)(2,1)S(1)}, u32[]{:S(2)}, u32[]{:S(2)}) collective-permute-start(bf16[3,24,4,64]{3,2,1,0:T(4,128)(2,1)S(1)} %get-tuple-element.519), channel_id=1, source_target_pairs={{0,1},{1,2},{2,3},{3,4},{4,5},{5,6},{6,7},{7,8},{8,9},{9,10},{10,1... | collective-permute-start | bytes 110600 | tf_op jit(solution)/shard_map/ppermute | solution.py:30
  350.7 4.0 fusion.164
  354.7 5.1 collective-permute-start.2
  373.9 5.1 all-to-all-start.5
  379.0 14.6 %collective-permute-done.2 = bf16[48,1,128,128]{3,2,1,0:T(8,128)(2,1)} collective-permute-done((bf16[48,1,128,128]{3,2,1,0:T(8,128)(2,1)}, bf16[48,1,128,128]{3,2,1,0:T(8,128)(2,1)}, u32[]{:S(2)}, u32[]{:S(2)}) %collective-permute-start.2) | collective-permute-done | bytes 1572896 | tf_op jit(solution)/shard_map/ppermute | solution.py:30
  393.7 3.6 copy.146
  400.0 3.6 copy.147
  405.6 6.2 all-to-all-start.6
  411.8 13.3 %pad_maximum_fusion.1 = bf16[6,8,10,128,128]{4,1,3,2,0:T(8,128)(2,1)} fusion(bf16[6,8,1,128,128]{4,1,3,2,0:T(8,128)(2,1)} %copy.147, bf16[6,8,8,128,128]{4,1,3,2,0:T(8,128)(2,1)} %get-tuple-element.241, bf16[6,8,1,128,128]{4,1,3,2,0:T(8,128)(2,1)} %copy.146), kind=kLoop, calls=%fused_computation.97 | loop fusion | flops 15728640 | bytes 31457280 | tf_op jit(solution)/shard_map/concatenate | solution.py:28
  427.0 145.8 %while.29 = (s32[]{:T(128)}, f32[4,8,128,128]{3,0,2,1:T(4,128)}, f32[6,8]{1,0:T(8,128)S(1)}, f32[6,8]{1,0:T(8,128)S(1)}, f32[6,8]{1,0:T(8,128)S(1)}, /*index=5*/...) while((s32[]{:T(128)}, f32[4,8,128,128]{3,0,2,1:T(4,128)}, ...), condition=%wide.region_7.8_spmd.clone, body=%wide.region_6.7_spmd.clone.sunk | while | flops 76808344 | bytes 55575712 | solution.py:213
  434.6 16.7 %select_add_fusion.5 = f32[4,8,128,128]{3,0,2,1:T(4,128)} fusion(f32[4,8,128,128]{3,0,2,1:T(4,128)} %get-tuple-element.730, f32[8,8,128,128]{3,0,2,1:T(8,128)} %slice.1269, f32[8,10,128,128]{3,0,2,1:T(8,128)} %copy-done.1, f32[8,128,128]{2,1,0:T(8,128)} %copy.188, f32[8]{0:T(128)S(1)} %fusion.183, f32[8]{0:T(128)S(1)} %get-tuple-element.674, ...), kind=kOutput, calls=%fused_computation.62.clone.1 | convolution fusion | flops 75497568 | bytes 17301888 | tf_op jit(solution)/shard_map/while/body/eval_jaxpr/km,mzxy->kzxy/dot_general | solution.py:107
  458.9 16.7 %select_add_fusion.5 = f32[4,8,128,128]{3,0,2,1:T(4,128)} fusion(f32[4,8,128,128]{3,0,2,1:T(4,128)} %get-tuple-element.730, f32[8,8,128,128]{3,0,2,1:T(8,128)} %slice.1269, f32[8,10,128,128]{3,0,2,1:T(8,128)} %copy-done.1, f32[8,128,128]{2,1,0:T(8,128)} %copy.188, f32[8]{0:T(128)S(1)} %fusion.183, f32[8]{0:T(128)S(1)} %get-tuple-element.674, ...), kind=kOutput, calls=%fused_computation.62.clone.1 | convolution fusion | flops 75497568 | bytes 17301888 | tf_op jit(solution)/shard_map/while/body/eval_jaxpr/km,mzxy->kzxy/dot_general | solution.py:107
  483.2 16.7 %select_add_fusion.5 = f32[4,8,128,128]{3,0,2,1:T(4,128)} fusion(f32[4,8,128,128]{3,0,2,1:T(4,128)} %get-tuple-element.730, f32[8,8,128,128]{3,0,2,1:T(8,128)} %slice.1269, f32[8,10,128,128]{3,0,2,1:T(8,128)} %copy-done.1, f32[8,128,128]{2,1,0:T(8,128)} %copy.188, f32[8]{0:T(128)S(1)} %fusion.183, f32[8]{0:T(128)S(1)} %get-tuple-element.674, ...), kind=kOutput, calls=%fused_computation.62.clone.1 | convolution fusion | flops 75497568 | bytes 17301888 | tf_op jit(solution)/shard_map/while/body/eval_jaxpr/km,mzxy->kzxy/dot_general | solution.py:107
  507.5 16.7 %select_add_fusion.5 = f32[4,8,128,128]{3,0,2,1:T(4,128)} fusion(f32[4,8,128,128]{3,0,2,1:T(4,128)} %get-tuple-element.730, f32[8,8,128,128]{3,0,2,1:T(8,128)} %slice.1269, f32[8,10,128,128]{3,0,2,1:T(8,128)} %copy-done.1, f32[8,128,128]{2,1,0:T(8,128)} %copy.188, f32[8]{0:T(128)S(1)} %fusion.183, f32[8]{0:T(128)S(1)} %get-tuple-element.674, ...), kind=kOutput, calls=%fused_computation.62.clone.1 | convolution fusion | flops 75497568 | bytes 17301888 | tf_op jit(solution)/shard_map/while/body/eval_jaxpr/km,mzxy->kzxy/dot_general | solution.py:107
  531.8 16.7 %select_add_fusion.5 = f32[4,8,128,128]{3,0,2,1:T(4,128)} fusion(f32[4,8,128,128]{3,0,2,1:T(4,128)} %get-tuple-element.730, f32[8,8,128,128]{3,0,2,1:T(8,128)} %slice.1269, f32[8,10,128,128]{3,0,2,1:T(8,128)} %copy-done.1, f32[8,128,128]{2,1,0:T(8,128)} %copy.188, f32[8]{0:T(128)S(1)} %fusion.183, f32[8]{0:T(128)S(1)} %get-tuple-element.674, ...), kind=kOutput, calls=%fused_computation.62.clone.1 | convolution fusion | flops 75497568 | bytes 17301888 | tf_op jit(solution)/shard_map/while/body/eval_jaxpr/km,mzxy->kzxy/dot_general | solution.py:107
  556.1 16.7 %select_add_fusion.5 = f32[4,8,128,128]{3,0,2,1:T(4,128)} fusion(f32[4,8,128,128]{3,0,2,1:T(4,128)} %get-tuple-element.730, f32[8,8,128,128]{3,0,2,1:T(8,128)} %slice.1269, f32[8,10,128,128]{3,0,2,1:T(8,128)} %copy-done.1, f32[8,128,128]{2,1,0:T(8,128)} %copy.188, f32[8]{0:T(128)S(1)} %fusion.183, f32[8]{0:T(128)S(1)} %get-tuple-element.674, ...), kind=kOutput, calls=%fused_computation.62.clone.1 | convolution fusion | flops 75497568 | bytes 17301888 | tf_op jit(solution)/shard_map/while/body/eval_jaxpr/km,mzxy->kzxy/dot_general | solution.py:107
  577.6 34.0 %all_to_all.92 = f32[16,4,8,128,8]{3,4,2,1,0:T(8,128)} all-to-all(f32[16,4,8,128,8]{3,4,2,1,0:T(8,128)S(1)} %copy.162), channel_id=1, replica_groups=mesh['space'=8,'mode'=16] {'mode'}, dimensions={0} | all-to-all | bytes 4194304 | tf_op jit(solution)/shard_map/all_to_all | solution.py:56
  618.8 7.6 %all_to_all.93 = f32[8,1,4096]{2,1,0:T(1,128)S(1)} all-to-all(f32[8,1,4096]{2,1,0:T(1,128)S(1)} %reshape.270), channel_id=1, replica_groups=mesh['space'=8,'mode'=16] {'space'}, dimensions={0} | all-to-all | bytes 262144 | tf_op jit(solution)/shard_map/all_to_all | solution.py:250
  635.5 3.5 collective-permute-start.12
  641.3 5.8 collective-permute-done.12
  648.4 3.9 collective-permute-done.13
  652.7 6.4 collective-permute-start.14
  (288 shorter events, 209.0 us)
Async XLA Ops:
  0.6 9.4 %copy-start.5 = (f32[16,8,64]{2,1,0:T(8,128)S(1)}, f32[16,8,64]{2,1,0:T(8,128)}, u32[]{:S(2)}) copy-start(f32[16,8,64]{2,1,0:T(8,128)} %param.14) | copy-start | bytes 98308
  0.6 16.8 %copy-start.13 = (s32[48]{0:T(128)S(1)}, s32[48]{0:T(128)}, u32[]{:S(2)}) copy-start(s32[48]{0:T(128)} %param.17) | copy-start | bytes 580
  0.7 16.8 %copy-start.12 = (f32[6]{0:T(128)S(1)}, f32[6]{0:T(128)}, u32[]{:S(2)}) copy-start(f32[6]{0:T(128)} %param.19) | copy-start | bytes 76
  0.7 16.9 %copy-start.9 = (s32[48]{0:T(128)S(1)}, s32[48]{0:T(128)}, u32[]{:S(2)}) copy-start(s32[48]{0:T(128)} %param.18) | copy-start | bytes 580
  0.7 59.2 %copy-start.10 = (f32[48]{0:T(128)S(1)}, f32[48]{0:T(128)}, u32[]{:S(2)}) copy-start(f32[48]{0:T(128)} %param.15) | copy-start | bytes 580
  0.7 59.2 %copy-start.11 = (f32[48]{0:T(128)S(1)}, f32[48]{0:T(128)}, u32[]{:S(2)}) copy-start(f32[48]{0:T(128)} %param.16) | copy-start | bytes 580
  4.7 71.8 %collective-permute-start = (bf16[48,1,128,128]{3,2,1,0:T(8,128)(2,1)}, bf16[48,1,128,128]{3,2,1,0:T(8,128)(2,1)}, u32[]{:S(2)}, u32[]{:S(2)}) collective-permute-start(bf16[48,1,128,128]{3,2,1,0:T(8,128)(2,1)} %get-tuple-element.499), channel_id=1, source_target_pairs={{0,16},{16,32},{32,48},{48,64},{64,80},{80,96},{96,112},{1,17},{17... | collective-permute-start | bytes 4718600 | tf_op jit(solution)/shard_map/ppermute | solution.py:30
  8.1 68.4 %collective-permute-start.1 = (bf16[48,1,128,128]{3,2,1,0:T(8,128)(2,1)}, bf16[48,1,128,128]{3,2,1,0:T(8,128)(2,1)}, u32[]{:S(2)}, u32[]{:S(2)}) collective-permute-start(bf16[48,1,128,128]{3,2,1,0:T(8,128)(2,1)} %get-tuple-element.500), channel_id=1, source_target_pairs={{16,0},{32,16},{48,32},{64,48},{80,64},{96,80},{112,96},{17,1},{33... | collective-permute-start | bytes 4718600 | tf_op jit(solution)/shard_map/ppermute | solution.py:32
  11.0 36.7 %all-to-all-start = ((f32[8,1,1024]{2,1,0:T(1,128)}), f32[8,1,1024]{2,1,0:T(1,128)S(1)}, u32[]{:S(2)}, u32[]{:S(2)}) async-start(f32[8,1,1024]{2,1,0:T(1,128)} %reshape.264), calls=%async_computation | async-start | bytes 65536 | tf_op jit(solution)/shard_map/all_to_all | solution.py:187
  50.3 19.2 %all-to-all-start.1 = ((f32[16,8,128,8]{2,3,1,0:T(8,128)}), f32[16,8,128,8]{2,3,1,0:T(8,128)S(1)}, u32[]{:S(2)}, u32[]{:S(2)}) async-start(f32[16,8,128,8]{2,3,1,0:T(8,128)} %stack.19), calls=%async_computation.1 | async-start | bytes 1048576 | tf_op jit(solution)/shard_map/all_to_all | solution.py:18
  70.8 196.4 %all-to-all-start.4 = ((f32[16,1,1]{2,1,0:T(1,128)}), f32[16,1,1]{2,1,0:T(1,128)S(1)}, u32[]{:S(2)}, u32[]{:S(2)}) async-start(f32[16,1,1]{2,1,0:T(1,128)} %broadcast_in_dim.50), calls=%async_computation.4 | async-start | bytes 16384 | tf_op jit(solution)/shard_map/all_to_all | solution.py:41
  93.6 3.7 copy-start
  122.3 3.7 copy-start
  151.0 3.7 copy-start
  179.7 3.7 copy-start
  208.4 3.7 copy-start
  237.1 3.7 copy-start
  262.0 5.2 copy-start.8
  263.9 10.5 %copy-start.6 = (f32[16,8,64]{2,1,0:T(8,128)S(1)}, f32[16,8,64]{2,1,0:T(8,128)}, u32[]{:S(2)}) copy-start(f32[16,8,64]{2,1,0:T(8,128)} %param.20) | copy-start | bytes 98308
  263.9 10.5 %copy-start.7 = (s32[16,8,64]{2,1,0:T(8,128)S(1)}, s32[16,8,64]{2,1,0:T(8,128)}, u32[]{:S(2)}) copy-start(s32[16,8,64]{2,1,0:T(8,128)} %param.21) | copy-start | bytes 98308
  267.2 34.1 %all-to-all-start.2 = ((f32[16,4,8,128,8]{3,4,2,1,0:T(8,128)}), f32[16,4,8,128,8]{3,4,2,1,0:T(8,128)S(1)}, u32[]{:S(2)}, u32[]{:S(2)}) async-start(f32[16,4,8,128,8]{3,4,2,1,0:T(8,128)} %copy.149), calls=%async_computation.2 | async-start | bytes 4194304 | tf_op jit(solution)/shard_map/all_to_all | solution.py:56
  274.5 5.3 collective-permute-start.8
  276.4 7.2 %collective-permute-start.9 = (bf16[4,8,64]{2,1,0:T(8,128)(2,1)S(1)}, bf16[4,8,64]{2,1,0:T(8,128)(2,1)S(1)}, u32[]{:S(2)}, u32[]{:S(2)}) collective-permute-start(bf16[4,8,64]{2,1,0:T(8,128)(2,1)S(1)} %get-tuple-element.524), channel_id=1, source_target_pairs={{16,0},{32,16},{48,32},{64,48},{80,64},{96,80},{112,96},{17,1},{33... | collective-permute-start | bytes 12296 | tf_op jit(solution)/shard_map/ppermute | solution.py:32
  283.7 25.2 %collective-permute-start.10 = (bf16[24,4,64]{2,1,0:T(4,128)(2,1)S(1)}, bf16[24,4,64]{2,1,0:T(4,128)(2,1)S(1)}, u32[]{:S(2)}, u32[]{:S(2)}) collective-permute-start(bf16[24,4,64]{2,1,0:T(4,128)(2,1)S(1)} %get-tuple-element.521), channel_id=1, source_target_pairs={{0,1},{1,2},{2,3},{3,4},{4,5},{5,6},{6,7},{7,8},{8,9},{9,10},{10,1... | collective-permute-start | bytes 36872 | tf_op jit(solution)/shard_map/ppermute | solution.py:30
  289.5 19.4 %collective-permute-start.11 = (bf16[24,4,64]{2,1,0:T(4,128)(2,1)S(1)}, bf16[24,4,64]{2,1,0:T(4,128)(2,1)S(1)}, u32[]{:S(2)}, u32[]{:S(2)}) collective-permute-start(bf16[24,4,64]{2,1,0:T(4,128)(2,1)S(1)} %get-tuple-element.522), channel_id=1, source_target_pairs={{1,0},{2,1},{3,2},{4,3},{5,4},{6,5},{7,6},{8,7},{9,8},{10,9},{11,1... | collective-permute-start | bytes 36872 | tf_op jit(solution)/shard_map/ppermute | solution.py:32
  304.9 7.9 %all-to-all-start.3 = ((f32[8,1,4096]{2,1,0:T(1,128)}), f32[8,1,4096]{2,1,0:T(1,128)S(1)}, u32[]{:S(2)}, u32[]{:S(2)}) async-start(f32[8,1,4096]{2,1,0:T(1,128)} %reshape.266), calls=%async_computation.3 | async-start | bytes 262144 | tf_op jit(solution)/shard_map/all_to_all | solution.py:250
  319.5 20.3 %collective-permute-start.4 = (bf16[3,4,8,64]{1,2,3,0:T(8,128)(2,1)}, bf16[3,4,8,64]{1,2,3,0:T(8,128)(2,1)}, u32[]{:S(2)}, u32[]{:S(2)}) collective-permute-start(bf16[3,4,8,64]{1,2,3,0:T(8,128)(2,1)} %get-tuple-element.513), channel_id=1, source_target_pairs={{0,16},{16,32},{32,48},{48,64},{64,80},{80,96},{96,112},{1,17},{17... | collective-permute-start | bytes 36872 | tf_op jit(solution)/shard_map/ppermute | solution.py:30
  322.9 18.2 %collective-permute-start.5 = (bf16[3,4,8,64]{1,2,3,0:T(8,128)(2,1)}, bf16[3,4,8,64]{1,2,3,0:T(8,128)(2,1)S(1)}, u32[]{:S(2)}, u32[]{:S(2)}) collective-permute-start(bf16[3,4,8,64]{1,2,3,0:T(8,128)(2,1)} %get-tuple-element.514), channel_id=1, source_target_pairs={{16,0},{32,16},{48,32},{64,48},{80,64},{96,80},{112,96},{17,1},{33... | collective-permute-start | bytes 36872 | tf_op jit(solution)/shard_map/ppermute | solution.py:32
  341.5 20.4 %collective-permute-start.6 = (bf16[3,24,4,64]{3,2,1,0:T(4,128)(2,1)S(1)}, bf16[3,24,4,64]{3,2,1,0:T(4,128)(2,1)S(1)}, u32[]{:S(2)}, u32[]{:S(2)}) collective-permute-start(bf16[3,24,4,64]{3,2,1,0:T(4,128)(2,1)S(1)} %get-tuple-element.519), channel_id=1, source_target_pairs={{0,1},{1,2},{2,3},{3,4},{4,5},{5,6},{6,7},{7,8},{8,9},{9,10},{10,1... | collective-permute-start | bytes 110600 | tf_op jit(solution)/shard_map/ppermute | solution.py:30
  348.8 13.1 %collective-permute-start.7 = (bf16[3,24,4,64]{3,2,1,0:T(4,128)(2,1)S(1)}, bf16[3,24,4,64]{3,2,1,0:T(4,128)(2,1)S(1)}, u32[]{:S(2)}, u32[]{:S(2)}) collective-permute-start(bf16[3,24,4,64]{3,2,1,0:T(4,128)(2,1)S(1)} %get-tuple-element.520), channel_id=1, source_target_pairs={{1,0},{2,1},{3,2},{4,3},{5,4},{6,5},{7,6},{8,7},{9,8},{10,9},{11,1... | collective-permute-start | bytes 110600 | tf_op jit(solution)/shard_map/ppermute | solution.py:32
  354.7 39.0 %collective-permute-start.2 = (bf16[48,1,128,128]{3,2,1,0:T(8,128)(2,1)}, bf16[48,1,128,128]{3,2,1,0:T(8,128)(2,1)}, u32[]{:S(2)}, u32[]{:S(2)}) collective-permute-start(bf16[48,1,128,128]{3,2,1,0:T(8,128)(2,1)} %get-tuple-element.497), channel_id=1, source_target_pairs={{0,16},{16,32},{32,48},{48,64},{64,80},{80,96},{96,112},{1,17},{17... | collective-permute-start | bytes 4718600 | tf_op jit(solution)/shard_map/ppermute | solution.py:30
  359.8 40.2 %collective-permute-start.3 = (bf16[48,1,128,128]{3,2,1,0:T(8,128)(2,1)}, bf16[48,1,128,128]{3,2,1,0:T(8,128)(2,1)}, u32[]{:S(2)}, u32[]{:S(2)}) collective-permute-start(bf16[48,1,128,128]{3,2,1,0:T(8,128)(2,1)} %get-tuple-element.498), channel_id=1, source_target_pairs={{16,0},{32,16},{48,32},{64,48},{80,64},{96,80},{112,96},{17,1},{33... | collective-permute-start | bytes 4718600 | tf_op jit(solution)/shard_map/ppermute | solution.py:32
  365.0 1.0 copy-start.2
  373.9 29.7 %all-to-all-start.5 = ((f32[8,1,1024]{2,1,0:T(1,128)}), f32[8,1,1024]{2,1,0:T(1,128)S(1)}, u32[]{:S(2)}, u32[]{:S(2)}) async-start(f32[8,1,1024]{2,1,0:T(1,128)} %reshape.268), calls=%async_computation.5 | async-start | bytes 65536 | tf_op jit(solution)/shard_map/all_to_all | solution.py:187
  405.6 19.5 %all-to-all-start.6 = ((f32[16,8,128,8]{2,3,1,0:T(8,128)}), f32[16,8,128,8]{2,3,1,0:T(8,128)S(1)}, u32[]{:S(2)}, u32[]{:S(2)}) async-start(f32[16,8,128,8]{2,3,1,0:T(8,128)} %stack.21), calls=%async_computation.6 | async-start | bytes 1048576 | tf_op jit(solution)/shard_map/all_to_all | solution.py:18
  425.1 0.8 copy-start.4
  429.2 3.7 copy-start.1
  453.5 3.7 copy-start.1
  477.8 3.7 copy-start.1
  502.1 3.7 copy-start.1
  526.4 3.7 copy-start.1
  550.7 3.7 copy-start.1
  635.5 11.6 %collective-permute-start.12 = (bf16[3,4,8,64]{1,2,3,0:T(8,128)(2,1)}, bf16[3,4,8,64]{1,2,3,0:T(8,128)(2,1)}, u32[]{:S(2)}, u32[]{:S(2)}) collective-permute-start(bf16[3,4,8,64]{1,2,3,0:T(8,128)(2,1)} %get-tuple-element.515), channel_id=1, source_target_pairs={{0,16},{16,32},{32,48},{48,64},{64,80},{80,96},{96,112},{1,17},{17... | collective-permute-start | bytes 36872 | tf_op jit(solution)/shard_map/ppermute | solution.py:30
  639.0 13.2 %collective-permute-start.13 = (bf16[3,4,8,64]{1,2,3,0:T(8,128)(2,1)}, bf16[3,4,8,64]{1,2,3,0:T(8,128)(2,1)S(1)}, u32[]{:S(2)}, u32[]{:S(2)}) collective-permute-start(bf16[3,4,8,64]{1,2,3,0:T(8,128)(2,1)} %get-tuple-element.516), channel_id=1, source_target_pairs={{16,0},{32,16},{48,32},{64,48},{80,64},{96,80},{112,96},{17,1},{33... | collective-permute-start | bytes 36872 | tf_op jit(solution)/shard_map/ppermute | solution.py:32
  652.7 12.6 %collective-permute-start.14 = (bf16[3,24,4,64]{3,2,1,0:T(4,128)(2,1)S(1)}, bf16[3,24,4,64]{3,2,1,0:T(4,128)(2,1)S(1)}, u32[]{:S(2)}, u32[]{:S(2)}) collective-permute-start(bf16[3,24,4,64]{3,2,1,0:T(4,128)(2,1)S(1)} %get-tuple-element.517), channel_id=1, source_target_pairs={{0,1},{1,2},{2,3},{3,4},{4,5},{5,6},{6,7},{7,8},{8,9},{9,10},{10,1... | collective-permute-start | bytes 110600 | tf_op jit(solution)/shard_map/ppermute | solution.py:30
  659.1 9.3 %collective-permute-start.15 = (bf16[3,24,4,64]{3,2,1,0:T(4,128)(2,1)S(1)}, bf16[3,24,4,64]{3,2,1,0:T(4,128)(2,1)S(1)}, u32[]{:S(2)}, u32[]{:S(2)}) collective-permute-start(bf16[3,24,4,64]{3,2,1,0:T(4,128)(2,1)S(1)} %get-tuple-element.518), channel_id=1, source_target_pairs={{1,0},{2,1},{3,2},{4,3},{5,4},{6,5},{7,6},{8,7},{9,8},{10,9},{11,1... | collective-permute-start | bytes 110600 | tf_op jit(solution)/shard_map/ppermute | solution.py:32
  671.4 1.0 copy-start.3
